TPU v7x, 32 devices: a whole 2x2x4 slice. The times are simulated.
32 devices in a mesh: row: 8 (over y, x, core), col: 4 (over z).
Axes of the slice: x: 2, y: 2, z: 4, core: 2. Of those that a mesh axis runs over, the one named last changes fastest.
Arguments:
- vectors: float32 [16384, 16384], P('row', 'col'), may hold values from -0.046875 to 0.046875
- basis: float32 [16384, 2048], P('col', 'row'), may hold values from -9 to 9
- block_units: int32 [8], replicated, may hold values from 1 to 40, 64 in all
Outputs:
- assembled: float32 [16384, 2048], P('row', 'col')
Inputs may be any that keep to these rules, and one draw needn't show every extreme that they name: `block_units`: the block sizes are whole numbers of units that sum to 64; the largest is exactly the maximum.
All inputs are finite; a program needn't handle non-finite values.
Results may differ from a plain program's by a relative error of at most 0.00007.
Values sent between devices are 32-bit elements; how exact they have to be, the bound alone decides.
A program may use at most 192 MiB of HBM per device.

v0:
```python
import jax
import jax.numpy as jnp
from jax import lax
from jax.sharding import PartitionSpec as P

UNIT = 256
START = 7168
LANES = 128


def block_ids(positions, block_units):
    ends = jnp.cumsum(block_units) * UNIT
    return jnp.sum((positions[:, None] >= ends[None, :-1]).astype(jnp.int32), axis=1)


def shards(vectors, basis, block_units):
    inner, width = basis.shape
    row_block = block_ids(
        lax.axis_index("col") * inner + jnp.arange(inner, dtype=jnp.int32), block_units
    )
    slab_block = block_ids(
        START + lax.axis_index("row") * width + jnp.arange(width, dtype=jnp.int32), block_units
    )
    masked = jnp.where(row_block[:, None] == slab_block[None, :], basis, jnp.float32(0.0))
    rows, cols = (lax.axis_size("row"), lax.axis_size("col"))
    step = LANES if width % LANES == 0 and rows % cols == 0 else width
    pieces = [
        lax.all_gather(masked[:, at : at + step], "row", axis=1, tiled=True)
        for at in range(0, width, step)
    ]
    sums = []
    for piece in pieces:
        part = jnp.dot(
            vectors, piece, precision=lax.Precision.HIGH, preferred_element_type=jnp.float32
        )
        sums.append(lax.psum_scatter(part, "col", scatter_dimension=1, tiled=True))
    groups = sums[0].shape[1] // step
    return jnp.concatenate(
        [one[:, g * step : (g + 1) * step] for g in range(groups) for one in sums], axis=1
    )


def solution(mesh):
    in_specs = (P("row", "col"), P("col", "row"), P())
    out_specs = P("row", "col")
    return jax.shard_map(shards, mesh=mesh, in_specs=in_specs, out_specs=out_specs, check_vma=False)
```

profile of v0, /device:TPU:0, one launch (start us, length us, event | category | flops | bytes accessed | tf_op | source)
XLA Modules:
  0.0 529.0 jit_solution(5976717857978838351)
XLA Ops:
  6.5 0.0 all-gather.3.cloned.1.call-start
  6.5 0.8 reduce-window.9
  7.4 0.1 convert_reduce_fusion.1
  7.5 0.1 convert_reduce_fusion
  7.6 3.9 compare_select_fusion
  11.5 2.3 fusion
  13.8 0.0 all-gather.3.cloned.1.call-update
  13.9 0.0 all-gather.5.cloned.1.call-start
  13.9 0.7 all-gather.5.cloned.1.call-update
  14.6 0.0 reduce-scatter.3.cloned.1.call-start
  14.7 95.1 %all-gather.3.cloned.1.call-done = f32[4096,1024]{1,0:T(8,128)} async-done(((f32[4096,128]{1,0:T(8,128)}), f32[4096,1024]{1,0:T(8,128)}) %all-gather.3.cloned.1.call-update) | async-done | bytes 16777232 | tf_op jit(solution)/shard_map/all_gather | solution.py:28
  109.8 111.0 %convolution_bitcast_fusion.1 = f32[2048,1024]{0,1:T(8,128)} fusion(f32[4096,1024]{1,0:T(8,128)} %all-gather.3.cloned.1.call-done, f32[2048,4096]{1,0:T(8,128)} %param.3), kind=kOutput, calls=%fused_computation.1 | convolution fusion | flops 51539607552 | bytes 58720256 | tf_op jit(solution)/shard_map/dot_general | solution.py:33
  220.7 0.0 reduce-scatter.3.cloned.1.call-update
  220.8 0.0 reduce-scatter.5.cloned.1.call-start
  220.8 0.0 all-gather.5.cloned.1.call-done
  220.8 111.1 %convolution_bitcast_fusion = f32[2048,1024]{0,1:T(8,128)} fusion(f32[4096,1024]{1,0:T(8,128)} %all-gather.5.cloned.1.call-done, f32[2048,4096]{1,0:T(8,128)} %param.3), kind=kOutput, calls=%fused_computation | convolution fusion | flops 51539607552 | bytes 58720256 | tf_op jit(solution)/shard_map/dot_general | solution.py:33
  332.0 0.0 reduce-scatter.5.cloned.1.call-update
  332.0 33.5 %reduce-scatter.3.cloned.1.call-done = f32[2048,256]{0,1:T(8,128)} async-done(((f32[2048,1024]{0,1:T(8,128)}), f32[2048,256]{0,1:T(8,128)}) %reduce-scatter.3.cloned.1.call-update) | async-done | bytes 2097168 | tf_op jit(solution)/shard_map/reduce_scatter | solution.py:36
  365.5 1.7 fusion.1
  367.2 145.8 %reduce-scatter.5.cloned.1.call-done = f32[2048,256]{0,1:T(8,128)} async-done(((f32[2048,1024]{0,1:T(8,128)}), f32[2048,256]{0,1:T(8,128)}) %reduce-scatter.5.cloned.1.call-update) | async-done | bytes 2097168 | tf_op jit(solution)/shard_map/reduce_scatter | solution.py:36
  513.0 1.8 fusion.2
  514.8 2.3 pad_maximum_fusion
  517.1 5.3 %copy.5 = f32[2048,512]{1,0:T(8,128)} copy(f32[2048,512]{0,1:T(8,128)} %pad_maximum_fusion) | data formatting | bytes 8388608 | tf_op jit(solution)/shard_map/concatenate | solution.py:38
  (4 shorter events, 0.0 us)
Async XLA Ops:
  6.5 103.2 %all-gather.3.cloned.1.call-start = ((), (), s32[]{:S(2)}) async-start(), calls=%async_computation.2 | async-start | bytes 18874368 | tf_op jit(solution)/shard_map/all_gather | solution.py:28
  13.9 207.0 %all-gather.5.cloned.1.call-start = ((), (), s32[]{:S(2)}) async-start(), calls=%async_computation.4 | async-start | bytes 18874368 | tf_op jit(solution)/shard_map/all_gather | solution.py:28
  14.6 350.9 %reduce-scatter.3.cloned.1.call-start = ((), (), s32[]{:S(2)}) async-start(), calls=%async_computation.3 | async-start | bytes 10485760 | tf_op jit(solution)/shard_map/reduce_scatter | solution.py:36
  220.8 292.2 %reduce-scatter.5.cloned.1.call-start = ((), (), s32[]{:S(2)}) async-start(), calls=%async_computation.5 | async-start | bytes 10485760 | tf_op jit(solution)/shard_map/reduce_scatter | solution.py:36
Sparse Core Ops, SparseCore 0:
  14.0 95.7 all-gather.2
  111.6 93.0 all-gather.4
  220.9 144.6 reduce-scatter.2
  367.7 145.2 reduce-scatter.4
where the time goes:
time: 529 us
  waiting for transfers between devices  275 us (52%)
  matrix products  222 us (42%)
  between operations  13.2 us (2%)
  local copies, waits for them, and re-layouts  11.1 us (2%)
  other arithmetic  7.3 us (1%)
    dot_general x2, matrix products, shards(): jnp.dot(vectors, piece, precision=lax.Precision.HIGH, preferred_element_t...  222 us
    reduce_scatter x2, waiting for transfers between devices, shards(): sums.append(lax.psum_scatter(part, 'col', scatter_dimension=1, tiled=True))  179 us
    all_gather x2, waiting for transfers between devices, shards(): lax.all_gather(masked[:, at:at + step], 'row', axis=1, tiled=True)  95.1 us
  transfers between devices with their start and end apart: 4, of which 3 were waited for; matrix products, arithmetic and copies ran while one was open for 42% of the time, Pallas kernels for 0%

commit v1 on v0

--- a/solution.py
+++ b/solution.py
@@ -25,7 +25,7 @@
     rows, cols = (lax.axis_size("row"), lax.axis_size("col"))
     step = LANES if width % LANES == 0 and rows % cols == 0 else width
     pieces = [
-        lax.all_gather(masked[:, at : at + step], "row", axis=1, tiled=True)
+        jnp.concatenate(lax.all_gather(masked[:, at : at + step], "row"), axis=1)
         for at in range(0, width, step)
     ]
     sums = []

time: 529 us -> 509 us (0.962)
  matrix products: 222 us -> 119 us
  waiting for transfers between devices: 275 us -> 322 us
  local copies, waits for them, and re-layouts: 11.1 us -> 46.6 us
    dot_general x2, matrix products: 222 us -> 119 us  [shards(): jnp.dot(vectors, piece, precision=lax.Precision.HIGH, preferred_element_t...]
    reduce_scatter x2, waiting for transfers between devices: 179 us -> 215 us  [shards(): sums.append(lax.psum_scatter(part, 'col', scatter_dimension=1, tiled=True))]
    reshape x0 -> x2, local copies, waits for them, and re-layouts: none -> 35.5 us  [shards(): jnp.concatenate(lax.all_gather(masked[:, at:at + step], 'row'), axis=1)]
    all_gather x2, waiting for transfers between devices: 95.1 us -> 106 us  [shards(): lax.all_gather(masked[:, at:at + step], 'row')]
  transfers between devices with their start and end apart: 4 -> 4, of which waited for: 3 -> 4; matrix products, arithmetic and copies ran while one was open for 42% -> 31% of each run, Pallas kernels for 0% -> 0%
where the time goes in v1:
time: 509 us
  waiting for transfers between devices  322 us (63%)
  matrix products  119 us (23%)
  local copies, waits for them, and re-layouts  46.6 us (9%)
  between operations  13.2 us (3%)
  other arithmetic  7.3 us (1%)
    reduce_scatter x2, waiting for transfers between devices, shards(): sums.append(lax.psum_scatter(part, 'col', scatter_dimension=1, tiled=True))  215 us
    dot_general x2, matrix products, shards(): jnp.dot(vectors, piece, precision=lax.Precision.HIGH, preferred_element_t...  119 us
    all_gather x2, waiting for transfers between devices, shards(): lax.all_gather(masked[:, at:at + step], 'row')  106 us
    reshape x2, local copies, waits for them, and re-layouts, shards(): jnp.concatenate(lax.all_gather(masked[:, at:at + step], 'row'), axis=1)  35.5 us
  transfers between devices with their start and end apart: 4, of which 4 were waited for; matrix products, arithmetic and copies ran while one was open for 31% of the time, Pallas kernels for 0%

profile of v1, /device:TPU:0, one launch (start us, length us, event | category | flops | bytes accessed | tf_op | source)
XLA Modules:
  0.0 508.6 jit_solution(12102702186903524368)
XLA Ops:
  6.5 0.0 all-gather.5.cloned.1.call-start
  6.5 0.8 reduce-window.9
  7.4 0.1 convert_reduce_fusion.1
  7.5 0.1 convert_reduce_fusion
  7.6 3.9 compare_select_fusion
  11.5 2.3 fusion
  13.8 0.0 all-gather.5.cloned.1.call-update
  13.8 0.0 all-gather.7.cloned.1.call-start
  13.9 0.7 all-gather.7.cloned.1.call-update
  14.6 0.0 reduce-scatter.3.cloned.1.call-start
  14.6 91.8 %all-gather.5.cloned.1.call-done = f32[32768,128]{1,0:T(8,128)} async-done(((f32[4096,128]{1,0:T(8,128)}), f32[32768,128]{1,0:T(8,128)}) %all-gather.5.cloned.1.call-update) | async-done | bytes 16777232 | tf_op jit(solution)/shard_map/all_gather | solution.py:28
  106.5 17.9 %copy.9 = f32[4096,8,128]{0,2,1:T(8,128)} copy(f32[4096,8,128]{2,0,1:T(8,128)} %bitcast.20) | data formatting | bytes 33554432 | tf_op jit(solution)/shard_map/reshape | solution.py:28
  124.4 59.7 %convolution_bitcast_fusion.1 = f32[2048,1024]{0,1:T(8,128)} fusion(f32[4096,1024]{0,1:T(8,128)} %bitcast.21, f32[2048,4096]{1,0:T(8,128)} %param.3), kind=kOutput, calls=%fused_computation.1 | convolution fusion | flops 51539607552 | bytes 58720256 | tf_op jit(solution)/shard_map/dot_general | solution.py:33
  184.1 0.0 reduce-scatter.3.cloned.1.call-update
  184.1 0.2 reduce-scatter.5.cloned.1.call-start
  184.3 13.8 %all-gather.7.cloned.1.call-done = f32[32768,128]{1,0:T(8,128)} async-done(((f32[4096,128]{1,0:T(8,128)}), f32[32768,128]{1,0:T(8,128)}) %all-gather.7.cloned.1.call-update) | async-done | bytes 16777232 | tf_op jit(solution)/shard_map/all_gather | solution.py:28
  198.1 17.6 %copy.10 = f32[4096,8,128]{0,2,1:T(8,128)} copy(f32[4096,8,128]{2,0,1:T(8,128)} %bitcast.19) | data formatting | bytes 33554432 | tf_op jit(solution)/shard_map/reshape | solution.py:28
  215.7 59.7 %convolution_bitcast_fusion = f32[2048,1024]{0,1:T(8,128)} fusion(f32[4096,1024]{0,1:T(8,128)} %bitcast.22, f32[2048,4096]{1,0:T(8,128)} %param.3), kind=kOutput, calls=%fused_computation | convolution fusion | flops 51539607552 | bytes 58720256 | tf_op jit(solution)/shard_map/dot_general | solution.py:33
  275.4 0.0 reduce-scatter.5.cloned.1.call-update
  275.4 69.7 %reduce-scatter.3.cloned.1.call-done = f32[2048,256]{0,1:T(8,128)} async-done(((f32[2048,1024]{0,1:T(8,128)}), f32[2048,256]{0,1:T(8,128)}) %reduce-scatter.3.cloned.1.call-update) | async-done | bytes 2097168 | tf_op jit(solution)/shard_map/reduce_scatter | solution.py:36
  345.1 1.7 fusion.1
  346.8 145.8 %reduce-scatter.5.cloned.1.call-done = f32[2048,256]{0,1:T(8,128)} async-done(((f32[2048,1024]{0,1:T(8,128)}), f32[2048,256]{0,1:T(8,128)}) %reduce-scatter.5.cloned.1.call-update) | async-done | bytes 2097168 | tf_op jit(solution)/shard_map/reduce_scatter | solution.py:36
  492.6 1.8 fusion.2
  494.3 2.3 pad_maximum_fusion
  496.7 5.3 %copy.11 = f32[2048,512]{1,0:T(8,128)} copy(f32[2048,512]{0,1:T(8,128)} %pad_maximum_fusion) | data formatting | bytes 8388608 | tf_op jit(solution)/shard_map/concatenate | solution.py:38
  (4 shorter events, 0.0 us)
Async XLA Ops:
  6.5 99.9 %all-gather.5.cloned.1.call-start = ((), (), s32[]{:S(2)}) async-start(), calls=%async_computation.4 | async-start | bytes 18874368 | tf_op jit(solution)/shard_map/all_gather | solution.py:28
  13.8 184.3 %all-gather.7.cloned.1.call-start = ((), (), s32[]{:S(2)}) async-start(), calls=%async_computation.5 | async-start | bytes 18874368 | tf_op jit(solution)/shard_map/all_gather | solution.py:28
  14.6 330.5 %reduce-scatter.3.cloned.1.call-start = ((), (), s32[]{:S(2)}) async-start(), calls=%async_computation.2 | async-start | bytes 10485760 | tf_op jit(solution)/shard_map/reduce_scatter | solution.py:36
  184.1 308.5 %reduce-scatter.5.cloned.1.call-start = ((), (), s32[]{:S(2)}) async-start(), calls=%async_computation.3 | async-start | bytes 10485760 | tf_op jit(solution)/shard_map/reduce_scatter | solution.py:36
Sparse Core Ops, SparseCore 0:
  14.0 92.4 all-gather.4
  108.3 89.7 all-gather.6
  200.5 144.6 reduce-scatter.2
  347.3 145.2 reduce-scatter.4
